TPU v7x, 256 devices: a whole 4x4x8 slice. The times are simulated.
256 devices in a mesh: unit: 4 (over y_lo, core), zero: 32 (over z, y_hi, x_hi), cols: 2 (over x_lo).
Axes of the slice: x: 4 (x_hi: 2, x_lo: 2; x = x_hi * 2 + x_lo), y: 4 (y_hi: 2, y_lo: 2; y = y_hi * 2 + y_lo), z: 8, core: 2. Of those that a mesh axis runs over, the one named last changes fastest.
Arguments:
- weight_gate: bfloat16 [20480, 13824], P(('unit', 'zero'), 'cols'), parts along dimension 0, may hold values from -0.15625 to 0.15625
- low_gate: bfloat16 [20480, 32], P(('unit', 'zero')), parts along dimension 0, may hold values from -0.078125 to 0.078125
- high_gate: bfloat16 [128, 13824], P('unit', 'cols'), parts along dimension 0, may hold values from -1 to 1
- weight_up: bfloat16 [20480, 13824], P(('unit', 'zero'), 'cols'), parts along dimension 0, may hold values from -0.15625 to 0.15625
- low_up: bfloat16 [20480, 32], P(('unit', 'zero')), parts along dimension 0, may hold values from -0.078125 to 0.078125
- high_up: bfloat16 [128, 13824], P('unit', 'cols'), parts along dimension 0, may hold values from -1 to 1
- norm_train: float32 [20480], P(('unit', 'zero', 'cols')), parts along dimension 0, may hold values from 0.25 to 1.75
- norm_step: float32 [20480], P(('unit', 'zero', 'cols')), parts along dimension 0, may hold values from -0.3 to 0.3
Outputs:
- final_gate: bfloat16 [20480, 13824], P('unit', ('cols', 'zero')), parts along dimension 0
- final_up: bfloat16 [20480, 13824], P('unit', ('cols', 'zero')), parts along dimension 0
- scale_gate: float32 [55296], P(('unit', 'cols', 'zero')), parts along dimension 0
- scale_up: float32 [55296], P(('unit', 'cols', 'zero')), parts along dimension 0
- serve_norm: bfloat16 [20480], P('unit'), parts along dimension 0
There are 4 independent parts, one for each index of `unit`. A program takes and returns all parts, laid end to end along the dimension named above; each array names one. Nothing has to cross between parts.
All inputs are finite; a program needn't handle non-finite values. Where the computation divides by a largest or mean magnitude, that divisor is 1e-20 or more.
Results may differ from a plain program's by a relative error of at most 0.001.
Values may be sent and summed in bfloat16 or wider, within the bound.
No kernel may reach another device: no remote copies, remote signals or barrier semaphores. Data moves between devices by JAX's collectives and lax.ppermute only.
A program may use at most 128 MiB of HBM per device.

v0:
```python
import jax
import jax.numpy as jnp
from jax import lax
from jax.sharding import PartitionSpec as P

D_MODEL = 5120
mix_rate = 0.5


def copy_for_each(value, axis):
    copies = jnp.broadcast_to(value, (lax.axis_size(axis), *value.shape))
    return lax.all_to_all(copies, axis, split_axis=0, concat_axis=0, tiled=True)


def over_copies(value, axis):
    return copy_for_each(value, axis).sum(axis=0)


def together(arrays, axis):
    vector, at, outs = (jnp.concatenate([a.reshape(-1) for a in arrays]), 0, [])
    total = over_copies(vector, axis)
    for a in arrays:
        outs.append(total[at : at + a.size].reshape(a.shape))
        at += a.size
    return tuple(outs)


def laid_out(blocks, dim):
    blocks = jnp.moveaxis(blocks, 0, dim)
    dims = blocks.shape
    return blocks.reshape(*dims[:dim], dims[dim] * dims[dim + 1], *dims[dim + 2 :])


def gathered_copies(value, axis, dim):
    return laid_out(copy_for_each(value, axis), dim)


def local(weight_gate, low_gate, high_gate, weight_up, low_up, high_up, norm_train, norm_step):
    result_gate = weight_gate.astype(jnp.float32) + mix_rate * jnp.dot(
        low_gate, high_gate, preferred_element_type=jnp.float32
    )
    result_up = weight_up.astype(jnp.float32) + mix_rate * jnp.dot(
        low_up, high_up, preferred_element_type=jnp.float32
    )
    total_gate, total_up = together(
        (jnp.sum(jnp.abs(result_gate), axis=0), jnp.sum(jnp.abs(result_up), axis=0)), "zero"
    )
    scale_gate = total_gate / D_MODEL
    scale_up = total_up / D_MODEL
    narrow_gate, narrow_up = (
        (result_gate / scale_gate).astype(jnp.bfloat16),
        (result_up / scale_up).astype(jnp.bfloat16),
    )
    final_gate, final_up = (
        lax.all_to_all(narrow_gate, "zero", split_axis=1, concat_axis=0, tiled=True),
        lax.all_to_all(narrow_up, "zero", split_axis=1, concat_axis=0, tiled=True),
    )
    place = lax.axis_index("zero")
    scale_gate = lax.dynamic_slice_in_dim(
        scale_gate, place * final_gate.shape[1], final_gate.shape[1]
    )
    scale_up = lax.dynamic_slice_in_dim(scale_up, place * final_up.shape[1], final_up.shape[1])
    serve_norm = gathered_copies((norm_train + norm_step).astype(jnp.bfloat16), ("zero", "cols"), 0)
    return (final_gate, final_up, scale_gate, scale_up, serve_norm)


def solution(mesh):
    in_specs = (
        P(("unit", "zero"), "cols"),
        P(("unit", "zero"), None),
        P("unit", "cols"),
        P(("unit", "zero"), "cols"),
        P(("unit", "zero"), None),
        P("unit", "cols"),
        P(("unit", "zero", "cols")),
        P(("unit", "zero", "cols")),
    )
    out_specs = (
        P("unit", ("cols", "zero")),
        P("unit", ("cols", "zero")),
        P(("unit", "cols", "zero")),
        P(("unit", "cols", "zero")),
        P("unit"),
    )
    return jax.shard_map(local, mesh=mesh, in_specs=in_specs, out_specs=out_specs, check_vma=False)
```

profile of v0, /device:TPU:64, one launch (start us, length us, event | category | flops | bytes accessed | tf_op | source)
XLA Modules:
  0.0 244.0 jit_solution(5626973775937074867)
XLA Ops:
  0.6 0.0 copy-start
  0.6 0.0 copy-start.2
  0.7 0.0 copy-start.1
  0.7 0.0 copy-start.3
  0.7 1.0 copy-done
  1.7 4.7 %abs_reduce_fusion = (f32[6912]{0:T(1024)S(1)}, f32[160,6912]{1,0:T(8,128)}) fusion(bf16[160,32]{0,1:T(8,128)(2,1)} %param.12, bf16[32,6912]{1,0:T(8,128)(2,1)S(1)} %copy-done, bf16[160,6912]{1,0:T(8,128)(2,1)} %param.11), kind=kOutput, calls=%fused_computation.6 | convolution fusion | flops 76301568 | bytes 7115776 | tf_op jit(solution)/shard_map/dot_general | solution.py:42
  6.3 0.0 copy-done.2
  6.3 0.0 copy-done.1
  6.3 0.0 copy-done.3
  6.3 3.1 %abs_reduce_fusion.1 = (f32[6912]{0:T(1024)S(1)}, f32[160,6912]{1,0:T(8,128)}) fusion(bf16[160,32]{0,1:T(8,128)(2,1)S(1)} %copy-done.3, bf16[32,6912]{1,0:T(8,128)(2,1)S(1)} %copy-done.2, bf16[160,6912]{1,0:T(8,128)(2,1)S(1)} %copy-done.1), kind=kOutput, calls=%fused_computation.7 | convolution fusion | flops 76301568 | bytes 7115776 | tf_op jit(solution)/shard_map/dot_general | solution.py:39
  9.4 0.0 copy-start.4
  9.4 0.0 copy-start.5
  9.4 2.1 broadcast_in_dim.8
  11.6 13.4 %all-to-all-start = ((f32[32,1,13824]{2,1,0:T(1,128)}), f32[32,1,13824]{2,1,0:T(1,128)S(1)}, u32[]{:S(2)}, u32[]{:S(2)}) async-start(f32[32,1,13824]{2,1,0:T(1,128)} %broadcast_in_dim.8), calls=%async_computation | async-start | bytes 3538944 | tf_op jit(solution)/shard_map/all_to_all | solution.py:12
  24.9 0.0 copy-done.4
  24.9 0.0 copy-done.5
  25.0 45.9 %all-to-all-done = f32[32,1,13824]{2,1,0:T(1,128)S(1)} async-done(((f32[32,1,13824]{2,1,0:T(1,128)}), f32[32,1,13824]{2,1,0:T(1,128)S(1)}, u32[]{:S(2)}, u32[]{:S(2)}) %all-to-all-start) | async-done | bytes 1769504 | tf_op jit(solution)/shard_map/all_to_all | solution.py:12
  70.9 0.6 broadcast_in_dim.9
  71.5 5.4 %all-to-all-start.3 = ((bf16[64,1,80]{2,1,0:T(2,128)(2,1)}), bf16[64,1,80]{2,1,0:T(2,128)(2,1)S(1)}, u32[]{:S(2)}, u32[]{:S(2)}) async-start(bf16[64,1,80]{2,1,0:T(2,128)(2,1)} %broadcast_in_dim.9), calls=%async_computation.3 | async-start | bytes 65536 | tf_op jit(solution)/shard_map/all_to_all | solution.py:12
  76.9 1.0 reduce_sum.29
  77.9 6.2 %divide_convert_fusion = (bf16[160,6912]{1,0:T(8,128)(2,1)}, bf16[160,6912]{1,0:T(8,128)(2,1)}) fusion(f32[160,6912]{1,0:T(8,128)} %get-tuple-element.28, f32[6912]{0:T(1024)S(1)} %get-tuple-element.25, f32[160,6912]{1,0:T(8,128)} %get-tuple-element.30, f32[6912]{0:T(1024)S(1)} %get-tuple-element.26), kind=kLoop, calls=%fused_computation.4 | loop fusion | flops 4423680 | bytes 13326336 | tf_op jit(solution)/shard_map/convert_element_type | solution.py:52
  84.1 9.0 %all_to_all.37 = bf16[160,32,216]{2,1,0:T(8,128)(2,1)S(1)} reshape(bf16[160,6912]{1,0:T(8,128)(2,1)} %get-tuple-element.32) | data formatting | bytes 4423680 | tf_op jit(solution)/shard_map/all_to_all | solution.py:55
  93.2 3.0 %copy.28 = bf16[160,32,216]{2,0,1:T(8,128)(2,1)} copy(bf16[160,32,216]{2,1,0:T(8,128)(2,1)S(1)} %all_to_all.37) | data formatting | bytes 4423680 | tf_op jit(solution)/shard_map/all_to_all | solution.py:55
  96.2 0.0 all-to-all-done.3
  96.2 12.3 %all-to-all-start.1 = ((bf16[160,32,216]{2,0,1:T(8,128)(2,1)}), bf16[160,32,216]{2,0,1:T(8,128)(2,1)S(1)}, u32[]{:S(2)}, u32[]{:S(2)}) async-start(bf16[160,32,216]{2,0,1:T(8,128)(2,1)} %copy.28), calls=%async_computation.1 | async-start | bytes 5242880 | tf_op jit(solution)/shard_map/all_to_all | solution.py:55
  108.5 9.9 %all_to_all.41 = bf16[160,32,216]{2,1,0:T(8,128)(2,1)} reshape(bf16[160,6912]{1,0:T(8,128)(2,1)} %get-tuple-element.31) | data formatting | bytes 4423680 | tf_op jit(solution)/shard_map/all_to_all | solution.py:56
  118.4 4.7 %copy.29 = bf16[160,32,216]{2,0,1:T(8,128)(2,1)} copy(bf16[160,32,216]{2,1,0:T(8,128)(2,1)} %all_to_all.41) | data formatting | bytes 4423680 | tf_op jit(solution)/shard_map/all_to_all | solution.py:56
  123.1 48.5 %all-to-all-done.1 = bf16[160,32,216]{2,0,1:T(8,128)(2,1)S(1)} async-done(((bf16[160,32,216]{2,0,1:T(8,128)(2,1)}), bf16[160,32,216]{2,0,1:T(8,128)(2,1)S(1)}, u32[]{:S(2)}, u32[]{:S(2)}) %all-to-all-start.1) | async-done | bytes 2211872 | tf_op jit(solution)/shard_map/all_to_all | solution.py:55
  171.6 4.9 %all-to-all-start.2 = ((bf16[160,32,216]{2,0,1:T(8,128)(2,1)}), bf16[160,32,216]{2,0,1:T(8,128)(2,1)}, u32[]{:S(2)}, u32[]{:S(2)}) async-start(bf16[160,32,216]{2,0,1:T(8,128)(2,1)} %copy.29), calls=%async_computation.2 | async-start | bytes 5242880 | tf_op jit(solution)/shard_map/all_to_all | solution.py:56
  176.5 0.1 reduce.1
  176.6 0.7 reshape.30
  177.3 0.6 dynamic_slice.6
  178.0 0.6 dynamic_slice.7
  178.6 2.5 %copy.30 = bf16[5120,216]{0,1:T(8,128)(2,1)} copy(bf16[5120,216]{1,0:T(8,128)(2,1)S(1)} %bitcast.10) | data formatting | bytes 4423680
  181.1 58.6 %all-to-all-done.2 = bf16[160,32,216]{2,0,1:T(8,128)(2,1)} async-done(((bf16[160,32,216]{2,0,1:T(8,128)(2,1)}), bf16[160,32,216]{2,0,1:T(8,128)(2,1)}, u32[]{:S(2)}, u32[]{:S(2)}) %all-to-all-start.2) | async-done | bytes 2211872 | tf_op jit(solution)/shard_map/all_to_all | solution.py:56
  239.7 4.3 %copy.31 = bf16[5120,216]{0,1:T(8,128)(2,1)} copy(bf16[5120,216]{1,0:T(8,128)(2,1)} %bitcast.3) | data formatting | bytes 4423680
  (3 shorter events, 0.0 us)
Async XLA Ops:
  0.6 1.0 copy-start
  0.6 5.7 %copy-start.2 = (bf16[32,6912]{1,0:T(8,128)(2,1)S(1)}, bf16[32,6912]{1,0:T(8,128)(2,1)}, u32[]{:S(2)}) copy-start(bf16[32,6912]{1,0:T(8,128)(2,1)} %param.10) | copy-start | bytes 1327108
  0.7 5.7 %copy-start.1 = (bf16[160,6912]{1,0:T(8,128)(2,1)S(1)}, bf16[160,6912]{1,0:T(8,128)(2,1)}, u32[]{:S(2)}) copy-start(bf16[160,6912]{1,0:T(8,128)(2,1)} %param.8) | copy-start | bytes 6635524
  0.7 5.7 %copy-start.3 = (bf16[160,32]{0,1:T(8,128)(2,1)S(1)}, bf16[160,32]{0,1:T(8,128)(2,1)}, u32[]{:S(2)}) copy-start(bf16[160,32]{0,1:T(8,128)(2,1)} %param.9) | copy-start | bytes 30724
  9.4 15.5 %copy-start.4 = (f32[80]{0:T(128)S(1)}, f32[80]{0:T(128)}, u32[]{:S(2)}) copy-start(f32[80]{0:T(128)} %param.14) | copy-start | bytes 964
  9.4 15.5 %copy-start.5 = (f32[80]{0:T(128)S(1)}, f32[80]{0:T(128)}, u32[]{:S(2)}) copy-start(f32[80]{0:T(128)} %param.15) | copy-start | bytes 964
  11.6 59.3 %all-to-all-start = ((f32[32,1,13824]{2,1,0:T(1,128)}), f32[32,1,13824]{2,1,0:T(1,128)S(1)}, u32[]{:S(2)}, u32[]{:S(2)}) async-start(f32[32,1,13824]{2,1,0:T(1,128)} %broadcast_in_dim.8), calls=%async_computation | async-start | bytes 3538944 | tf_op jit(solution)/shard_map/all_to_all | solution.py:12
  71.5 24.7 %all-to-all-start.3 = ((bf16[64,1,80]{2,1,0:T(2,128)(2,1)}), bf16[64,1,80]{2,1,0:T(2,128)(2,1)S(1)}, u32[]{:S(2)}, u32[]{:S(2)}) async-start(bf16[64,1,80]{2,1,0:T(2,128)(2,1)} %broadcast_in_dim.9), calls=%async_computation.3 | async-start | bytes 65536 | tf_op jit(solution)/shard_map/all_to_all | solution.py:12
  96.2 75.4 %all-to-all-start.1 = ((bf16[160,32,216]{2,0,1:T(8,128)(2,1)}), bf16[160,32,216]{2,0,1:T(8,128)(2,1)S(1)}, u32[]{:S(2)}, u32[]{:S(2)}) async-start(bf16[160,32,216]{2,0,1:T(8,128)(2,1)} %copy.28), calls=%async_computation.1 | async-start | bytes 5242880 | tf_op jit(solution)/shard_map/all_to_all | solution.py:55
  171.6 68.1 %all-to-all-start.2 = ((bf16[160,32,216]{2,0,1:T(8,128)(2,1)}), bf16[160,32,216]{2,0,1:T(8,128)(2,1)}, u32[]{:S(2)}, u32[]{:S(2)}) async-start(bf16[160,32,216]{2,0,1:T(8,128)(2,1)} %copy.29), calls=%async_computation.2 | async-start | bytes 5242880 | tf_op jit(solution)/shard_map/all_to_all | solution.py:56
where the time goes:
time: 245 us; the launch traced here: 244 us
  waiting for transfers between devices  153 us (62%)
  local copies, waits for them, and re-layouts  39.1 us (16%)
  starting transfers between devices  35.9 us (15%)
  matrix products  7.76 us (3%)
  other arithmetic  7.35 us (3%)
    all_to_all x1, waiting for transfers between devices, local(): lax.all_to_all(narrow_up, 'zero', split_axis=1, concat_axis=0, tiled=True)  58.6 us
    all_to_all x1, waiting for transfers between devices, local(): lax.all_to_all(narrow_gate, 'zero', split_axis=1, concat_axis=0, tiled=True)  48.5 us
    all_to_all x2, waiting for transfers between devices, copy_for_each(): return lax.all_to_all(copies, axis, split_axis=0, concat_axis=0, tiled=True)  45.9 us
    all_to_all x2, starting transfers between devices, copy_for_each(): return lax.all_to_all(copies, axis, split_axis=0, concat_axis=0, tiled=True)  18.7 us
    all_to_all x2, local copies, waits for them, and re-layouts, local(): lax.all_to_all(narrow_up, 'zero', split_axis=1, concat_axis=0, tiled=True)  14.6 us
    all_to_all x1, starting transfers between devices, local(): lax.all_to_all(narrow_gate, 'zero', split_axis=1, concat_axis=0, tiled=True)  12.3 us
    all_to_all x2, local copies, waits for them, and re-layouts, local(): lax.all_to_all(narrow_gate, 'zero', split_axis=1, concat_axis=0, tiled=True)  12 us
    unnamed x14, local copies, waits for them, and re-layouts  7.74 us
  transfers between devices with their start and end apart: 4, of which 3 were waited for; matrix products, arithmetic and copies ran while one was open for 8% of the time, Pallas kernels for 0%

commit v1 on v0

--- a/solution.py
+++ b/solution.py
@@ -5,6 +5,13 @@
 
 D_MODEL = 5120
 mix_rate = 0.5
+
+
+def swap_blocks(x, axis, split, join):
+    count = lax.axis_size(axis)
+    pieces = jnp.stack(jnp.split(x, count, axis=split), axis=0)
+    pieces = lax.all_to_all(pieces, axis, split_axis=0, concat_axis=0)
+    return jnp.concatenate(pieces, axis=join)
 
 
 def copy_for_each(value, axis):
@@ -52,7 +59,7 @@
         (result_up / scale_up).astype(jnp.bfloat16),
     )
     final_gate, final_up = (
-        lax.all_to_all(narrow_gate, "zero", split_axis=1, concat_axis=0, tiled=True),
+        swap_blocks(narrow_gate, "zero", 1, 0),
         lax.all_to_all(narrow_up, "zero", split_axis=1, concat_axis=0, tiled=True),
     )
     place = lax.axis_index("zero")

time: 245 us -> 233 us (0.951)
  local copies, waits for them, and re-layouts: 39.1 us -> 31.4 us
    all_to_all x2 -> x0, local copies, waits for them, and re-layouts: 12 us -> none  [local(): lax.all_to_all(narrow_gate, 'zero', split_axis=1, concat_axis=0, tiled=True)]
    unnamed x14 -> x47, local copies, waits for them, and re-layouts: 7.74 us -> 11.9 us
    all_to_all x1, waiting for transfers between devices: 48.5 us -> 44.6 us  [swap_blocks(): pieces = lax.all_to_all(pieces, axis, split_axis=0, concat_axis=0)]
    convert_element_type x0 -> x1, other arithmetic: none -> 2.53 us  [local(): (result_gate / scale_gate).astype(jnp.bfloat16)]
  transfers between devices with their start and end apart: 4 -> 4, of which waited for: 3 -> 4; matrix products, arithmetic and copies ran while one was open for 8% -> 8% of each run, Pallas kernels for 0% -> 0%
where the time goes in v1:
time: 233 us
  waiting for transfers between devices  151 us (65%)
  starting transfers between devices  33.9 us (15%)
  local copies, waits for them, and re-layouts  31.4 us (13%)
  matrix products  7.79 us (3%)
  other arithmetic  7.53 us (3%)
    all_to_all x1, waiting for transfers between devices, local(): lax.all_to_all(narrow_up, 'zero', split_axis=1, concat_axis=0, tiled=True)  58.6 us
    all_to_all x2, waiting for transfers between devices, copy_for_each(): return lax.all_to_all(copies, axis, split_axis=0, concat_axis=0, tiled=True)  47.9 us
    all_to_all x1, waiting for transfers between devices, swap_blocks(): pieces = lax.all_to_all(pieces, axis, split_axis=0, concat_axis=0)  44.6 us
    all_to_all x2, starting transfers between devices, copy_for_each(): return lax.all_to_all(copies, axis, split_axis=0, concat_axis=0, tiled=True)  18.7 us
    all_to_all x2, local copies, waits for them, and re-layouts, local(): lax.all_to_all(narrow_up, 'zero', split_axis=1, concat_axis=0, tiled=True)  14.6 us
    unnamed x47, local copies, waits for them, and re-layouts  11.9 us
    all_to_all x1, starting transfers between devices, swap_blocks(): pieces = lax.all_to_all(pieces, axis, split_axis=0, concat_axis=0)  10.3 us
    all_to_all x1, starting transfers between devices, local(): lax.all_to_all(narrow_up, 'zero', split_axis=1, concat_axis=0, tiled=True)  4.89 us
  transfers between devices with their start and end apart: 4, of which 4 were waited for; matrix products, arithmetic and copies ran while one was open for 8% of the time, Pallas kernels for 0%

profile of v1, /device:TPU:64, one launch (start us, length us, event | category | flops | bytes accessed | tf_op | source)
XLA Modules:
  0.0 232.8 jit_solution(81916017146663212)
XLA Ops:
  0.6 0.0 copy-start
  0.6 0.0 copy-start.4
  0.7 0.0 copy-start.3
  0.7 0.0 copy-start.2
  0.7 1.0 copy-done
  1.7 4.7 %abs_reduce_fusion.1 = (f32[6912]{0:T(1024)S(1)}, f32[160,6912]{1,0:T(8,128)}) fusion(bf16[160,32]{0,1:T(8,128)(2,1)} %param.9, bf16[32,6912]{1,0:T(8,128)(2,1)S(1)} %copy-done, bf16[160,6912]{1,0:T(8,128)(2,1)} %param.8), kind=kOutput, calls=%fused_computation.7 | convolution fusion | flops 76301568 | bytes 7115776 | tf_op jit(solution)/shard_map/dot_general | solution.py:46
  6.4 0.0 copy-done.3
  6.4 3.1 %abs_reduce_fusion = (f32[6912]{0:T(1024)S(1)}, f32[160,6912]{1,0:T(8,128)}) fusion(bf16[160,32]{0,1:T(8,128)(2,1)S(1)} %copy-done.4, bf16[32,6912]{1,0:T(8,128)(2,1)S(1)} %copy-done.3, bf16[160,6912]{1,0:T(8,128)(2,1)S(1)} %copy-done.2), kind=kOutput, calls=%fused_computation.6 | convolution fusion | flops 76301568 | bytes 7115776 | tf_op jit(solution)/shard_map/dot_general | solution.py:49
  9.5 0.0 copy-start.6
  9.5 2.1 broadcast_in_dim.8
  11.6 13.4 %all-to-all-start = ((f32[32,1,13824]{2,1,0:T(1,128)}), f32[32,1,13824]{2,1,0:T(1,128)S(1)}, u32[]{:S(2)}, u32[]{:S(2)}) async-start(f32[32,1,13824]{2,1,0:T(1,128)} %broadcast_in_dim.8), calls=%async_computation | async-start | bytes 3538944 | tf_op jit(solution)/shard_map/all_to_all | solution.py:19
  25.0 0.0 copy-done.5
  25.0 0.0 copy-done.6
  25.0 45.9 %all-to-all-done = f32[32,1,13824]{2,1,0:T(1,128)S(1)} async-done(((f32[32,1,13824]{2,1,0:T(1,128)}), f32[32,1,13824]{2,1,0:T(1,128)S(1)}, u32[]{:S(2)}, u32[]{:S(2)}) %all-to-all-start) | async-done | bytes 1769504 | tf_op jit(solution)/shard_map/all_to_all | solution.py:19
  70.9 0.6 broadcast_in_dim.9
  71.6 5.4 %all-to-all-start.3 = ((bf16[64,1,80]{2,1,0:T(2,128)(2,1)}), bf16[64,1,80]{2,1,0:T(2,128)(2,1)S(1)}, u32[]{:S(2)}, u32[]{:S(2)}) async-start(bf16[64,1,80]{2,1,0:T(2,128)(2,1)} %broadcast_in_dim.9), calls=%async_computation.3 | async-start | bytes 65536 | tf_op jit(solution)/shard_map/all_to_all | solution.py:19
  76.9 1.0 reduce_sum.29
  78.0 2.5 %divide_convert_fusion.1 = bf16[160,6912]{1,0:T(8,128)(2,1)S(1)} fusion(f32[160,6912]{1,0:T(8,128)} %get-tuple-element.35, f32[6912]{0:T(1024)S(1)} %get-tuple-element.31), kind=kLoop, calls=%fused_computation.5 | loop fusion | flops 2211840 | bytes 6663168 | tf_op jit(solution)/shard_map/convert_element_type | solution.py:58
  80.5 0.1 fusion.32
  80.6 0.1 fusion.31
  80.7 0.1 fusion.30
  80.8 0.1 fusion.29
  80.9 0.1 fusion.28
  81.0 0.1 fusion.27
  81.1 0.1 fusion.26
  81.2 0.1 fusion.25
  81.3 0.1 fusion.24
  81.4 0.1 fusion.23
  81.5 0.1 fusion.22
  81.6 0.1 fusion.21
  81.7 0.1 fusion.20
  81.8 0.1 fusion.19
  81.9 0.1 fusion.18
  82.0 0.1 fusion.16
  82.1 0.1 fusion.15
  82.2 0.1 fusion.14
  82.3 0.1 fusion.13
  82.4 0.1 fusion.12
  82.5 0.1 fusion.11
  82.6 0.1 fusion.10
  82.7 0.1 fusion.9
  82.8 0.1 fusion.8
  82.9 0.1 fusion.7
  83.0 0.1 fusion.6
  83.1 0.1 fusion.5
  83.2 0.1 fusion.4
  83.3 0.1 fusion.3
  83.4 0.1 fusion.2
  83.5 0.0 copy-start.1
  83.5 1.5 copy-done.1
  85.0 2.0 all-to-all-done.3
  87.0 10.3 %all-to-all-start.1 = ((bf16[32,160,216]{2,1,0:T(8,128)(2,1)}), bf16[32,160,216]{2,1,0:T(8,128)(2,1)S(1)}, u32[]{:S(2)}, u32[]{:S(2)}) async-start(bf16[32,160,216]{2,1,0:T(8,128)(2,1)} %copy-done.1), calls=%async_computation.1 | async-start | bytes 5242880 | tf_op jit(solution)/shard_map/all_to_all | solution.py:13
  97.3 3.9 %divide_convert_fusion = bf16[160,6912]{1,0:T(8,128)(2,1)} fusion(f32[160,6912]{1,0:T(8,128)} %get-tuple-element.33, f32[6912]{0:T(1024)S(1)} %get-tuple-element.30), kind=kLoop, calls=%fused_computation.4 | loop fusion | flops 2211840 | bytes 6663168 | tf_op jit(solution)/shard_map/convert_element_type | solution.py:59
  101.2 9.9 %all_to_all.27 = bf16[160,32,216]{2,1,0:T(8,128)(2,1)} reshape(bf16[160,6912]{1,0:T(8,128)(2,1)} %divide_convert_fusion) | data formatting | bytes 4423680 | tf_op jit(solution)/shard_map/all_to_all | solution.py:63
  111.1 4.7 %copy.25 = bf16[160,32,216]{2,0,1:T(8,128)(2,1)} copy(bf16[160,32,216]{2,1,0:T(8,128)(2,1)} %all_to_all.27) | data formatting | bytes 4423680 | tf_op jit(solution)/shard_map/all_to_all | solution.py:63
  115.8 44.6 %all-to-all-done.1 = bf16[32,160,216]{2,1,0:T(8,128)(2,1)S(1)} async-done(((bf16[32,160,216]{2,1,0:T(8,128)(2,1)}), bf16[32,160,216]{2,1,0:T(8,128)(2,1)S(1)}, u32[]{:S(2)}, u32[]{:S(2)}) %all-to-all-start.1) | async-done | bytes 2211872 | tf_op jit(solution)/shard_map/all_to_all | solution.py:13
  160.5 4.9 %all-to-all-start.2 = ((bf16[160,32,216]{2,0,1:T(8,128)(2,1)}), bf16[160,32,216]{2,0,1:T(8,128)(2,1)}, u32[]{:S(2)}, u32[]{:S(2)}) async-start(bf16[160,32,216]{2,0,1:T(8,128)(2,1)} %copy.25), calls=%async_computation.2 | async-start | bytes 5242880 | tf_op jit(solution)/shard_map/all_to_all | solution.py:63
  165.4 0.1 reduce.1
  165.5 0.7 reshape.31
  166.2 0.6 dynamic_slice.6
  166.8 0.6 dynamic_slice.7
  167.4 2.5 %copy.26 = bf16[5120,216]{0,1:T(8,128)(2,1)} copy(bf16[5120,216]{1,0:T(8,128)(2,1)S(1)} %bitcast.136) | data formatting | bytes 4423680
  169.9 58.6 %all-to-all-done.2 = bf16[160,32,216]{2,0,1:T(8,128)(2,1)} async-done(((bf16[160,32,216]{2,0,1:T(8,128)(2,1)}), bf16[160,32,216]{2,0,1:T(8,128)(2,1)}, u32[]{:S(2)}, u32[]{:S(2)}) %all-to-all-start.2) | async-done | bytes 2211872 | tf_op jit(solution)/shard_map/all_to_all | solution.py:63
  228.5 4.3 %copy.27 = bf16[5120,216]{0,1:T(8,128)(2,1)} copy(bf16[5120,216]{1,0:T(8,128)(2,1)} %bitcast.34) | data formatting | bytes 4423680
  (8 shorter events, 0.0 us)
Async XLA Ops:
  0.6 1.0 copy-start
  0.6 5.7 %copy-start.4 = (bf16[160,32]{0,1:T(8,128)(2,1)S(1)}, bf16[160,32]{0,1:T(8,128)(2,1)}, u32[]{:S(2)}) copy-start(bf16[160,32]{0,1:T(8,128)(2,1)} %param.12) | copy-start | bytes 30724
  0.7 5.7 %copy-start.3 = (bf16[32,6912]{1,0:T(8,128)(2,1)S(1)}, bf16[32,6912]{1,0:T(8,128)(2,1)}, u32[]{:S(2)}) copy-start(bf16[32,6912]{1,0:T(8,128)(2,1)} %param.13) | copy-start | bytes 1327108
  0.7 5.7 %copy-start.2 = (bf16[160,6912]{1,0:T(8,128)(2,1)S(1)}, bf16[160,6912]{1,0:T(8,128)(2,1)}, u32[]{:S(2)}) copy-start(bf16[160,6912]{1,0:T(8,128)(2,1)} %param.11) | copy-start | bytes 6635524
  9.5 15.5 %copy-start.5 = (f32[80]{0:T(128)S(1)}, f32[80]{0:T(128)}, u32[]{:S(2)}) copy-start(f32[80]{0:T(128)} %param.14) | copy-start | bytes 964
  9.5 15.5 %copy-start.6 = (f32[80]{0:T(128)S(1)}, f32[80]{0:T(128)}, u32[]{:S(2)}) copy-start(f32[80]{0:T(128)} %param.15) | copy-start | bytes 964
  11.6 59.3 %all-to-all-start = ((f32[32,1,13824]{2,1,0:T(1,128)}), f32[32,1,13824]{2,1,0:T(1,128)S(1)}, u32[]{:S(2)}, u32[]{:S(2)}) async-start(f32[32,1,13824]{2,1,0:T(1,128)} %broadcast_in_dim.8), calls=%async_computation | async-start | bytes 3538944 | tf_op jit(solution)/shard_map/all_to_all | solution.py:19
  71.6 15.4 %all-to-all-start.3 = ((bf16[64,1,80]{2,1,0:T(2,128)(2,1)}), bf16[64,1,80]{2,1,0:T(2,128)(2,1)S(1)}, u32[]{:S(2)}, u32[]{:S(2)}) async-start(bf16[64,1,80]{2,1,0:T(2,128)(2,1)} %broadcast_in_dim.9), calls=%async_computation.3 | async-start | bytes 65536 | tf_op jit(solution)/shard_map/all_to_all | solution.py:19
  83.5 1.5 copy-start.1
  87.0 73.4 %all-to-all-start.1 = ((bf16[32,160,216]{2,1,0:T(8,128)(2,1)}), bf16[32,160,216]{2,1,0:T(8,128)(2,1)S(1)}, u32[]{:S(2)}, u32[]{:S(2)}) async-start(bf16[32,160,216]{2,1,0:T(8,128)(2,1)} %copy-done.1), calls=%async_computation.1 | async-start | bytes 5242880 | tf_op jit(solution)/shard_map/all_to_all | solution.py:13
  160.5 68.1 %all-to-all-start.2 = ((bf16[160,32,216]{2,0,1:T(8,128)(2,1)}), bf16[160,32,216]{2,0,1:T(8,128)(2,1)}, u32[]{:S(2)}, u32[]{:S(2)}) async-start(bf16[160,32,216]{2,0,1:T(8,128)(2,1)} %copy.25), calls=%async_computation.2 | async-start | bytes 5242880 | tf_op jit(solution)/shard_map/all_to_all | solution.py:63
